TPU v7x, 256 devices: a whole 4x4x8 slice. The times are simulated.
256 devices in a mesh: seq: 128 (over z, y_hi, x, core), head: 2 (over y_lo).
Axes of the slice: x: 4, y: 4 (y_hi: 2, y_lo: 2; y = y_hi * 2 + y_lo), z: 8, core: 2. Of those that a mesh axis runs over, the one named last changes fastest.
Arguments:
- queries: bfloat16 [49152, 32, 128], P(('seq', 'head')), may hold values from -6 to 6
- keys: bfloat16 [49152, 8, 128], P('seq', 'head'), may hold values from -6 to 6
- values: bfloat16 [49152, 8, 128], P('seq', 'head'), may hold values from -1.5 to 1.5
- outputs: bfloat16 [49152, 32, 128], P(('seq', 'head')), may hold values from -1.5 to 1.5
- output_gradient: bfloat16 [49152, 32, 128], P(('seq', 'head')), may hold values from -24 to 24
- lse: float32 [49152, 32], P(('seq', 'head')), may hold values from 5.5 to 7.5
Outputs:
- query_grad: bfloat16 [49152, 32, 128], P(('seq', 'head'))
- key_gradient: bfloat16 [49152, 8, 128], P('seq', 'head')
- value_gradient: bfloat16 [49152, 8, 128], P('seq', 'head')
All inputs are finite; a program needn't handle non-finite values.
Results may differ from a plain program's by a relative error of at most 0.0068.
Values may be sent and summed in bfloat16 or wider, within the bound.
A program may use at most 64 MiB of HBM per device.

v0:
```python
import jax
import jax.numpy as jnp
from jax import lax
from jax.sharding import PartitionSpec as P


def shifted(shard, axis, by):
    size = lax.axis_size(axis)
    pairs = [(i, i + by) for i in range(size) if 0 <= i + by < size]
    return lax.ppermute(shard, axis, pairs)


def body(queries, keys, values, outputs, output_gradient, lse):
    row_delta = jnp.sum(output_gradient.astype(jnp.float32) * outputs.astype(jnp.float32), axis=-1)
    query_blk, grad_blk = (
        lax.all_to_all(queries, "head", split_axis=1, concat_axis=0, tiled=True),
        lax.all_to_all(output_gradient, "head", split_axis=1, concat_axis=0, tiled=True),
    )
    lse_blk, delta_blk = (
        lax.all_to_all(lse, "head", split_axis=1, concat_axis=0, tiled=True),
        lax.all_to_all(row_delta, "head", split_axis=1, concat_axis=0, tiled=True),
    )
    token_length = keys.shape[0]
    heads_kv = keys.shape[1]
    head_dim = keys.shape[2]
    heads_query = query_blk.shape[1]
    query_groups = heads_query // heads_kv
    score_scale = head_dim ** (-0.5)
    near_key, near_value = shifted((keys, values), "seq", 1)
    far_key, far_value = shifted((near_key, near_value), "seq", 1)
    key_cat = jnp.concatenate([far_key, near_key, keys], 0)
    value_cat = jnp.concatenate([far_value, near_value, values], 0)
    block_start = lax.axis_index("seq") * token_length
    row_ids = jnp.arange(token_length, dtype=jnp.int32)[:, None]
    col_ids = jnp.arange(3 * token_length, dtype=jnp.int32)[None, :]
    allowed = (
        (block_start - 2 * token_length + col_ids >= 0)
        & (col_ids > row_ids)
        & (col_ids <= row_ids + 2 * token_length)
    )
    query_four = query_blk.reshape(token_length, heads_kv, query_groups, head_dim)
    grad_four = grad_blk.reshape(token_length, heads_kv, query_groups, head_dim)
    lse_three = lse_blk.reshape(token_length, heads_kv, query_groups)
    delta_three = delta_blk.reshape(token_length, heads_kv, query_groups)
    query_list = []
    key_list = []
    value_list = []
    for group in range(heads_kv):
        query_one = query_four[:, group]
        grad_one = grad_four[:, group]
        lse_one = lse_three[:, group]
        delta_one = delta_three[:, group]
        key_one = key_cat[:, group]
        value_one = value_cat[:, group]
        scores = (
            jnp.einsum("tgd,cd->tgc", query_one, key_one, preferred_element_type=jnp.float32)
            * score_scale
        )
        attn_prob = jnp.where(allowed[:, None, :], jnp.exp(scores - lse_one[..., None]), 0.0)
        prob_bf = attn_prob.astype(jnp.bfloat16)
        val_part = jnp.einsum("tgc,tgd->cd", prob_bf, grad_one, preferred_element_type=jnp.float32)
        prob_grad = jnp.einsum(
            "tgd,cd->tgc", grad_one, value_one, preferred_element_type=jnp.float32
        )
        score_bf = (attn_prob * (prob_grad - delta_one[..., None]) * score_scale).astype(
            jnp.bfloat16
        )
        query_part = jnp.einsum(
            "tgc,cd->tgd", score_bf, key_one, preferred_element_type=jnp.float32
        ).astype(jnp.bfloat16)
        key_part = jnp.einsum(
            "tgc,tgd->cd", score_bf, query_one, preferred_element_type=jnp.float32
        )
        query_list.append(query_part)
        key_list.append(key_part)
        value_list.append(val_part)
    query_local = jnp.stack(query_list, 1).reshape(token_length, heads_query, head_dim)
    key_all = jnp.stack(key_list, 1)
    value_all = jnp.stack(value_list, 1)
    own_key = key_all[2 * token_length :]
    own_value = value_all[2 * token_length :]
    prev_key = key_all[token_length : 2 * token_length]
    prev_value = value_all[token_length : 2 * token_length]
    back_key = key_all[:token_length]
    back_value = value_all[:token_length]
    held_key, held_value = (
        shifted(back_key.astype(jnp.bfloat16), "seq", -1).astype(back_key.dtype),
        shifted(back_value.astype(jnp.bfloat16), "seq", -1).astype(back_value.dtype),
    )
    came_key, came_value = (
        shifted((prev_key + held_key).astype(jnp.bfloat16), "seq", -1).astype(jnp.float32),
        shifted((prev_value + held_value).astype(jnp.bfloat16), "seq", -1).astype(jnp.float32),
    )
    key_total = own_key + came_key
    value_total = own_value + came_value
    query_grad = lax.all_to_all(query_local, "head", split_axis=0, concat_axis=1, tiled=True)
    return (query_grad, key_total.astype(jnp.bfloat16), value_total.astype(jnp.bfloat16))


def solution(mesh):
    return jax.shard_map(
        body,
        mesh=mesh,
        in_specs=(
            P(("seq", "head"), None, None),
            P("seq", "head", None),
            P("seq", "head", None),
            P(("seq", "head"), None, None),
            P(("seq", "head"), None, None),
            P(("seq", "head"), None),
        ),
        out_specs=(P(("seq", "head"), None, None), P("seq", "head", None), P("seq", "head", None)),
        check_vma=False,
    )
```

profile of v0, /device:TPU:119, one launch (start us, length us, event | category | flops | bytes accessed | tf_op | source)
XLA Modules:
  0.0 153.7 jit_solution(1230618401118679281)
XLA Ops:
  0.6 3.4 %all-to-all-start.1 = ((f32[192,2,16]{0,2,1:T(8,128)}), f32[192,2,16]{0,2,1:T(8,128)S(1)}, u32[]{:S(2)}, u32[]{:S(2)}) async-start(f32[192,2,16]{0,2,1:T(8,128)} %bitcast.198), calls=%async_computation.1 | async-start | bytes 65536 | tf_op jit(solution)/shard_map/all_to_all | solution.py:20
  4.1 1.9 %copy.57 = bf16[384,4,128]{2,0,1:T(8,128)(2,1)} copy(bf16[384,4,128]{2,1,0:T(4,128)(2,1)} %param.8) | data formatting | bytes 786432 | tf_op args[2]
  6.0 5.0 %collective-permute-start.2 = (bf16[384,4,128]{2,0,1:T(8,128)(2,1)}, bf16[384,4,128]{2,0,1:T(8,128)(2,1)}, u32[]{:S(2)}, u32[]{:S(2)}) collective-permute-start(bf16[384,4,128]{2,0,1:T(8,128)(2,1)} %copy.57), channel_id=1, source_target_pairs={{0,2},{2,4},{4,6},{6,8},{8,10},{10,12},{12,14},{14,16},{16,18},{18... | collective-permute-start | bytes 1179656 | tf_op jit(solution)/shard_map/ppermute | solution.py:10
  12.8 1.9 %collective-permute-start = (bf16[384,4,128]{2,0,1:T(8,128)(2,1)}, bf16[384,4,128]{2,0,1:T(8,128)(2,1)}, u32[]{:S(2)}, u32[]{:S(2)}) collective-permute-start(bf16[384,4,128]{2,0,1:T(8,128)(2,1)} %copy.52), channel_id=1, source_target_pairs={{0,2},{2,4},{4,6},{6,8},{8,10},{10,12},{12,14},{14,16},{16,18},{18... | collective-permute-start | bytes 1179656 | tf_op jit(solution)/shard_map/ppermute | solution.py:10
  14.7 2.3 %multiply_reduce_fusion = f32[192,32]{1,0:T(8,128)S(1)} fusion(bf16[192,32,128]{2,1,0:T(8,128)(2,1)} %param.9, bf16[192,32,128]{2,1,0:T(8,128)(2,1)S(1)} %copy-done.1), kind=kLoop, calls=%fused_computation.24 | loop fusion | flops 3139584 | bytes 3170304 | tf_op jit(solution)/shard_map/reduce_sum | solution.py:14
  17.7 3.6 %all-to-all-start.3 = ((f32[192,2,16]{0,2,1:T(8,128)}), f32[192,2,16]{0,2,1:T(8,128)S(1)}, u32[]{:S(2)}, u32[]{:S(2)}) async-start(f32[192,2,16]{0,2,1:T(8,128)} %bitcast.16), calls=%async_computation.3 | async-start | bytes 65536 | tf_op jit(solution)/shard_map/all_to_all | solution.py:21
  24.6 3.7 %all-to-all-start = ((bf16[192,32,128]{2,0,1:T(8,128)(2,1)}), bf16[192,32,128]{2,0,1:T(8,128)(2,1)S(1)}, u32[]{:S(2)}, u32[]{:S(2)}) async-start(bf16[192,32,128]{2,0,1:T(8,128)(2,1)} %copy.54), calls=%async_computation | async-start | bytes 3145728 | tf_op jit(solution)/shard_map/all_to_all | solution.py:16
  29.4 1.8 %copy.59 = bf16[192,32,128]{2,0,1:T(8,128)(2,1)} copy(bf16[192,32,128]{2,1,0:T(8,128)(2,1)S(1)} %copy-done.1) | data formatting | bytes 3145728 | tf_op args[4]
  31.5 4.9 %collective-permute-start.1 = (bf16[384,4,128]{2,0,1:T(8,128)(2,1)}, bf16[384,4,128]{2,0,1:T(8,128)(2,1)S(1)}, u32[]{:S(2)}, u32[]{:S(2)}) collective-permute-start(bf16[384,4,128]{2,0,1:T(8,128)(2,1)} %collective-permute-done), channel_id=1, source_target_pairs={{0,2},{2,4},{4,6},{6,8},{8,10},{10,12},{12,14},{14,16},{16,18},{18... | collective-permute-start | bytes 1179656 | tf_op jit(solution)/shard_map/ppermute | solution.py:10
  37.0 2.0 %collective-permute-start.3 = (bf16[384,4,128]{2,0,1:T(8,128)(2,1)}, bf16[384,4,128]{2,0,1:T(8,128)(2,1)S(1)}, u32[]{:S(2)}, u32[]{:S(2)}) collective-permute-start(bf16[384,4,128]{2,0,1:T(8,128)(2,1)} %collective-permute-done.2), channel_id=1, source_target_pairs={{0,2},{2,4},{4,6},{6,8},{8,10},{10,12},{12,14},{14,16},{16,18},{18... | collective-permute-start | bytes 1179656 | tf_op jit(solution)/shard_map/ppermute | solution.py:10
  41.4 4.7 %all-to-all-done = bf16[192,32,128]{2,0,1:T(8,128)(2,1)S(1)} async-done(((bf16[192,32,128]{2,0,1:T(8,128)(2,1)}), bf16[192,32,128]{2,0,1:T(8,128)(2,1)S(1)}, u32[]{:S(2)}, u32[]{:S(2)}) %all-to-all-start) | async-done | bytes 1572896 | tf_op jit(solution)/shard_map/all_to_all | solution.py:16
  46.2 4.8 %all-to-all-start.2 = ((bf16[192,32,128]{2,0,1:T(8,128)(2,1)}), bf16[192,32,128]{2,0,1:T(8,128)(2,1)}, u32[]{:S(2)}, u32[]{:S(2)}) async-start(bf16[192,32,128]{2,0,1:T(8,128)(2,1)} %copy.59), calls=%async_computation.2 | async-start | bytes 3145728 | tf_op jit(solution)/shard_map/all_to_all | solution.py:17
  55.3 12.7 %all-to-all-done.2 = bf16[192,32,128]{2,0,1:T(8,128)(2,1)} async-done(((bf16[192,32,128]{2,0,1:T(8,128)(2,1)}), bf16[192,32,128]{2,0,1:T(8,128)(2,1)}, u32[]{:S(2)}, u32[]{:S(2)}) %all-to-all-start.2) | async-done | bytes 1572896 | tf_op jit(solution)/shard_map/all_to_all | solution.py:17
  71.5 1.9 %fusion.25 = f32[1152,1,128]{2,0,1:T(8,128)} fusion(f32[384,4,1152]{0,2,1:T(8,128)S(1)} %bitcast_select_fusion, bf16[384,4,4,128]{3,0,2,1:T(8,128)(2,1)S(1)} %bitcast.177), kind=kOutput, calls=%fused_computation.28 | convolution fusion | flops 454754304 | bytes 8060928 | tf_op jit(solution)/shard_map/tgc,tgd->cd/dot_general | solution.py:61
  76.8 1.8 %bitcast_select_fusion.1 = f32[384,4,1152]{0,2,1:T(8,128)S(1)} fusion(f32[384,4]{0,1:T(4,128)S(1)} %copy-done.19, pred[384,1152]{0,1:T(8,128)(4,1)S(1)} %copy-done.11, bf16[384,4,4,128]{3,0,2,1:T(8,128)(2,1)S(1)} %bitcast.188, bf16[1152,4,128]{2,0,1:T(8,128)(2,1)S(1)} %copy-done.14), kind=kOutput, calls=%fused_computation.7 | convolution fusion | flops 458293248 | bytes 8214528 | tf_op jit(solution)/shard_map/tgd,cd->tgc/dot_general | solution.py:56
  78.6 2.0 %fusion.22 = f32[1152,1,128]{2,0,1:T(8,128)} fusion(f32[384,4,1152]{0,2,1:T(8,128)S(1)} %bitcast_select_fusion.1, bf16[384,4,4,128]{3,0,2,1:T(8,128)(2,1)S(1)} %bitcast.179), kind=kOutput, calls=%fused_computation.27 | convolution fusion | flops 454754304 | bytes 8060928 | tf_op jit(solution)/shard_map/tgc,tgd->cd/dot_general | solution.py:61
  84.0 2.0 %bitcast_select_fusion.2 = f32[384,4,1152]{0,2,1:T(8,128)S(1)} fusion(f32[384,4]{0,1:T(4,128)S(1)} %copy-done.18, pred[384,1152]{0,1:T(8,128)(4,1)S(1)} %copy-done.12, bf16[384,4,4,128]{3,0,2,1:T(8,128)(2,1)S(1)} %bitcast.190, bf16[1152,4,128]{2,0,1:T(8,128)(2,1)S(1)} %copy-done.14), kind=kOutput, calls=%fused_computation.11 | convolution fusion | flops 458293248 | bytes 8214528 | tf_op jit(solution)/shard_map/tgd,cd->tgc/dot_general | solution.py:56
  86.1 1.9 %fusion.19 = f32[1152,1,128]{2,0,1:T(8,128)} fusion(f32[384,4,1152]{0,2,1:T(8,128)S(1)} %bitcast_select_fusion.2, bf16[384,4,4,128]{3,0,2,1:T(8,128)(2,1)S(1)} %bitcast.181), kind=kOutput, calls=%fused_computation.26 | convolution fusion | flops 454754304 | bytes 8060928 | tf_op jit(solution)/shard_map/tgc,tgd->cd/dot_general | solution.py:61
  90.3 1.9 %convolution_bitcast_fusion.2 = f32[1152,1,128]{2,0,1:T(8,128)} fusion(bf16[384,4,1152]{0,2,1:T(8,128)(2,1)S(1)} %fusion.5, bf16[384,4,4,128]{3,0,2,1:T(8,128)(2,1)S(1)} %bitcast.191), kind=kOutput, calls=%fused_computation.31 | convolution fusion | flops 452984832 | bytes 4521984 | tf_op jit(solution)/shard_map/tgc,tgd->cd/dot_general | solution.py:71
  94.1 1.9 %fusion.16 = f32[1152,1,128]{2,0,1:T(8,128)} fusion(f32[384,4,1152]{0,2,1:T(8,128)S(1)} %bitcast_select_fusion.3, bf16[384,4,4,128]{3,0,2,1:T(8,128)(2,1)S(1)} %bitcast.183), kind=kOutput, calls=%fused_computation.25 | convolution fusion | flops 454754304 | bytes 8060928 | tf_op jit(solution)/shard_map/tgc,tgd->cd/dot_general | solution.py:61
  97.1 1.9 %convolution_bitcast_fusion.3 = f32[1152,1,128]{2,0,1:T(8,128)} fusion(bf16[384,4,1152]{0,2,1:T(8,128)(2,1)S(1)} %fusion.7, bf16[384,4,4,128]{3,0,2,1:T(8,128)(2,1)S(1)} %bitcast.193), kind=kOutput, calls=%fused_computation.32 | convolution fusion | flops 452984832 | bytes 4521984 | tf_op jit(solution)/shard_map/tgc,tgd->cd/dot_general | solution.py:71
  100.4 2.2 %copy.67 = bf16[384,16,128]{2,1,0:T(8,128)(2,1)} copy(bf16[384,16,128]{2,0,1:T(8,128)(2,1)S(1)} %bitcast.194) | data formatting | bytes 3145728 | tf_op jit(solution)/shard_map/reshape | solution.py:77
  102.5 4.6 %all-to-all-start.4 = ((bf16[384,16,128]{2,1,0:T(8,128)(2,1)}), bf16[384,16,128]{2,1,0:T(8,128)(2,1)}, u32[]{:S(2)}, u32[]{:S(2)}) async-start(bf16[384,16,128]{2,1,0:T(8,128)(2,1)} %copy.67), calls=%async_computation.4 | async-start | bytes 3145728 | tf_op jit(solution)/shard_map/all_to_all | solution.py:96
  108.8 5.0 %collective-permute-start.4 = (bf16[384,4,128]{2,0,1:T(8,128)(2,1)S(1)}, bf16[384,4,128]{2,0,1:T(8,128)(2,1)S(1)}, u32[]{:S(2)}, u32[]{:S(2)}) collective-permute-start(bf16[384,4,128]{2,0,1:T(8,128)(2,1)S(1)} %slice.219), channel_id=1, source_target_pairs={{2,0},{4,2},{6,4},{8,6},{10,8},{12,10},{14,12},{16,14},{18,16},{20... | collective-permute-start | bytes 1179656 | tf_op jit(solution)/shard_map/ppermute | solution.py:10
  114.1 1.9 %collective-permute-start.6 = (bf16[384,4,128]{2,0,1:T(8,128)(2,1)S(1)}, bf16[384,4,128]{2,0,1:T(8,128)(2,1)S(1)}, u32[]{:S(2)}, u32[]{:S(2)}) collective-permute-start(bf16[384,4,128]{2,0,1:T(8,128)(2,1)S(1)} %slice.218), channel_id=1, source_target_pairs={{2,0},{4,2},{6,4},{8,6},{10,8},{12,10},{14,12},{16,14},{18,16},{20... | collective-permute-start | bytes 1179656 | tf_op jit(solution)/shard_map/ppermute | solution.py:10
  116.1 15.3 %collective-permute-done.4 = bf16[384,4,128]{2,0,1:T(8,128)(2,1)S(1)} collective-permute-done((bf16[384,4,128]{2,0,1:T(8,128)(2,1)S(1)}, bf16[384,4,128]{2,0,1:T(8,128)(2,1)S(1)}, u32[]{:S(2)}, u32[]{:S(2)}) %collective-permute-start.4) | collective-permute-done | bytes 393248 | tf_op jit(solution)/shard_map/ppermute | solution.py:10
  131.5 1.9 %collective-permute-start.5 = (bf16[384,4,128]{2,0,1:T(8,128)(2,1)S(1)}, bf16[384,4,128]{2,0,1:T(8,128)(2,1)S(1)}, u32[]{:S(2)}, u32[]{:S(2)}) collective-permute-start(bf16[384,4,128]{2,0,1:T(8,128)(2,1)S(1)} %fusion.36), channel_id=1, source_target_pairs={{2,0},{4,2},{6,4},{8,6},{10,8},{12,10},{14,12},{16,14},{18,16},{20... | collective-permute-start | bytes 1179656 | tf_op jit(solution)/shard_map/ppermute | solution.py:10
  133.4 2.2 %collective-permute-done.6 = bf16[384,4,128]{2,0,1:T(8,128)(2,1)S(1)} collective-permute-done((bf16[384,4,128]{2,0,1:T(8,128)(2,1)S(1)}, bf16[384,4,128]{2,0,1:T(8,128)(2,1)S(1)}, u32[]{:S(2)}, u32[]{:S(2)}) %collective-permute-start.6) | collective-permute-done | bytes 393248 | tf_op jit(solution)/shard_map/ppermute | solution.py:10
  136.4 1.9 %collective-permute-start.7 = (bf16[384,4,128]{2,0,1:T(8,128)(2,1)}, bf16[384,4,128]{2,0,1:T(8,128)(2,1)S(1)}, u32[]{:S(2)}, u32[]{:S(2)}) collective-permute-start(bf16[384,4,128]{2,0,1:T(8,128)(2,1)} %fusion.34), channel_id=1, source_target_pairs={{2,0},{4,2},{6,4},{8,6},{10,8},{12,10},{14,12},{16,14},{18,16},{20... | collective-permute-start | bytes 1179656 | tf_op jit(solution)/shard_map/ppermute | solution.py:10
  138.4 2.8 %copy.68 = bf16[192,2,16,128]{3,2,1,0:T(8,128)(2,1)} copy(bf16[192,2,16,128]{3,2,0,1:T(8,128)(2,1)} %bitcast.58) | data formatting | bytes 3145728 | tf_op jit(solution)/shard_map/all_to_all | solution.py:96
  141.2 5.1 %collective-permute-done.5 = bf16[384,4,128]{2,0,1:T(8,128)(2,1)S(1)} collective-permute-done((bf16[384,4,128]{2,0,1:T(8,128)(2,1)S(1)}, bf16[384,4,128]{2,0,1:T(8,128)(2,1)S(1)}, u32[]{:S(2)}, u32[]{:S(2)}) %collective-permute-start.5) | collective-permute-done | bytes 393248 | tf_op jit(solution)/shard_map/ppermute | solution.py:10
  147.4 4.0 %collective-permute-done.7 = bf16[384,4,128]{2,0,1:T(8,128)(2,1)S(1)} collective-permute-done((bf16[384,4,128]{2,0,1:T(8,128)(2,1)}, bf16[384,4,128]{2,0,1:T(8,128)(2,1)S(1)}, u32[]{:S(2)}, u32[]{:S(2)}) %collective-permute-start.7) | collective-permute-done | bytes 393248 | tf_op jit(solution)/shard_map/ppermute | solution.py:10
  (92 shorter events, 37.4 us)
Async XLA Ops:
  0.6 14.1 %copy-start.1 = (bf16[192,32,128]{2,1,0:T(8,128)(2,1)S(1)}, bf16[192,32,128]{2,1,0:T(8,128)(2,1)}, u32[]{:S(2)}) copy-start(bf16[192,32,128]{2,1,0:T(8,128)(2,1)} %param.10) | copy-start | bytes 4718596
  0.6 17.1 %all-to-all-start.1 = ((f32[192,2,16]{0,2,1:T(8,128)}), f32[192,2,16]{0,2,1:T(8,128)S(1)}, u32[]{:S(2)}, u32[]{:S(2)}) async-start(f32[192,2,16]{0,2,1:T(8,128)} %bitcast.198), calls=%async_computation.1 | async-start | bytes 65536 | tf_op jit(solution)/shard_map/all_to_all | solution.py:20
  4.0 17.3 %copy-start.8 = (bf16[192,32,128]{2,1,0:T(8,128)(2,1)S(1)}, bf16[192,32,128]{2,1,0:T(8,128)(2,1)}, u32[]{:S(2)}) copy-start(bf16[192,32,128]{2,1,0:T(8,128)(2,1)} %param.6) | copy-start | bytes 4718596
  6.0 31.0 %collective-permute-start.2 = (bf16[384,4,128]{2,0,1:T(8,128)(2,1)}, bf16[384,4,128]{2,0,1:T(8,128)(2,1)}, u32[]{:S(2)}, u32[]{:S(2)}) collective-permute-start(bf16[384,4,128]{2,0,1:T(8,128)(2,1)} %copy.57), channel_id=1, source_target_pairs={{0,2},{2,4},{4,6},{6,8},{8,10},{10,12},{12,14},{14,16},{16,18},{18... | collective-permute-start | bytes 1179656 | tf_op jit(solution)/shard_map/ppermute | solution.py:10
  12.8 18.7 %collective-permute-start = (bf16[384,4,128]{2,0,1:T(8,128)(2,1)}, bf16[384,4,128]{2,0,1:T(8,128)(2,1)}, u32[]{:S(2)}, u32[]{:S(2)}) collective-permute-start(bf16[384,4,128]{2,0,1:T(8,128)(2,1)} %copy.52), channel_id=1, source_target_pairs={{0,2},{2,4},{4,6},{6,8},{8,10},{10,12},{12,14},{14,16},{16,18},{18... | collective-permute-start | bytes 1179656 | tf_op jit(solution)/shard_map/ppermute | solution.py:10
  17.7 6.9 %all-to-all-start.3 = ((f32[192,2,16]{0,2,1:T(8,128)}), f32[192,2,16]{0,2,1:T(8,128)S(1)}, u32[]{:S(2)}, u32[]{:S(2)}) async-start(f32[192,2,16]{0,2,1:T(8,128)} %bitcast.16), calls=%async_computation.3 | async-start | bytes 65536 | tf_op jit(solution)/shard_map/all_to_all | solution.py:21
  24.6 21.6 %all-to-all-start = ((bf16[192,32,128]{2,0,1:T(8,128)(2,1)}), bf16[192,32,128]{2,0,1:T(8,128)(2,1)S(1)}, u32[]{:S(2)}, u32[]{:S(2)}) async-start(bf16[192,32,128]{2,0,1:T(8,128)(2,1)} %copy.54), calls=%async_computation | async-start | bytes 3145728 | tf_op jit(solution)/shard_map/all_to_all | solution.py:16
  31.5 9.9 %collective-permute-start.1 = (bf16[384,4,128]{2,0,1:T(8,128)(2,1)}, bf16[384,4,128]{2,0,1:T(8,128)(2,1)S(1)}, u32[]{:S(2)}, u32[]{:S(2)}) collective-permute-start(bf16[384,4,128]{2,0,1:T(8,128)(2,1)} %collective-permute-done), channel_id=1, source_target_pairs={{0,2},{2,4},{4,6},{6,8},{8,10},{10,12},{12,14},{14,16},{16,18},{18... | collective-permute-start | bytes 1179656 | tf_op jit(solution)/shard_map/ppermute | solution.py:10
  37.0 16.2 %collective-permute-start.3 = (bf16[384,4,128]{2,0,1:T(8,128)(2,1)}, bf16[384,4,128]{2,0,1:T(8,128)(2,1)S(1)}, u32[]{:S(2)}, u32[]{:S(2)}) collective-permute-start(bf16[384,4,128]{2,0,1:T(8,128)(2,1)} %collective-permute-done.2), channel_id=1, source_target_pairs={{0,2},{2,4},{4,6},{6,8},{8,10},{10,12},{12,14},{14,16},{16,18},{18... | collective-permute-start | bytes 1179656 | tf_op jit(solution)/shard_map/ppermute | solution.py:10
  46.2 21.7 %all-to-all-start.2 = ((bf16[192,32,128]{2,0,1:T(8,128)(2,1)}), bf16[192,32,128]{2,0,1:T(8,128)(2,1)}, u32[]{:S(2)}, u32[]{:S(2)}) async-start(bf16[192,32,128]{2,0,1:T(8,128)(2,1)} %copy.59), calls=%async_computation.2 | async-start | bytes 3145728 | tf_op jit(solution)/shard_map/all_to_all | solution.py:17
  53.0 1.3 copy-start.9
  53.0 2.1 %copy-start.10 = (bf16[384,4,128]{2,1,0:T(4,128)(2,1)S(1)}, bf16[384,4,128]{2,1,0:T(4,128)(2,1)}, u32[]{:S(2)}) copy-start(bf16[384,4,128]{2,1,0:T(4,128)(2,1)} %param.8) | copy-start | bytes 1179652
  54.3 15.2 %copy-start.11 = (pred[384,1152]{0,1:T(8,128)(4,1)S(1)}, pred[384,1152]{0,1:T(8,128)(4,1)}, u32[]{:S(2)}) copy-start(pred[384,1152]{0,1:T(8,128)(4,1)} %fusion.29) | copy-start | bytes 1327108
  54.3 15.2 %copy-start.20 = (f32[384,4]{0,1:T(4,128)S(1)}, f32[384,4]{0,1:T(4,128)}, u32[]{:S(2)}) copy-start(f32[384,4]{0,1:T(4,128)} %get-tuple-element.20) | copy-start | bytes 18436
  55.3 18.1 %copy-start.6 = (bf16[1152,4,128]{2,0,1:T(8,128)(2,1)}, bf16[1152,4,128]{2,0,1:T(8,128)(2,1)S(1)}, u32[]{:S(2)}) copy-start(bf16[1152,4,128]{2,0,1:T(8,128)(2,1)S(1)} %constant_dynamic-update-slice_fusion.3) | copy-start | bytes 3538948
  67.9 1.7 %copy-start.14 = (bf16[1152,4,128]{2,0,1:T(8,128)(2,1)S(1)}, bf16[1152,4,128]{2,0,1:T(8,128)(2,1)}, u32[]{:S(2)}) copy-start(bf16[1152,4,128]{2,0,1:T(8,128)(2,1)} %constant_dynamic-update-slice_fusion) | copy-start | bytes 3538948
  71.5 1.9 %copy-start.16 = (f32[384,4]{0,1:T(4,128)S(1)}, f32[384,4]{0,1:T(4,128)}, u32[]{:S(2)}) copy-start(f32[384,4]{0,1:T(4,128)} %get-tuple-element.16) | copy-start | bytes 18436
  78.6 2.0 %copy-start.7 = (bf16[1152,4,128]{2,0,1:T(8,128)(2,1)S(1)}, bf16[1152,4,128]{2,0,1:T(8,128)(2,1)}, u32[]{:S(2)}) copy-start(bf16[1152,4,128]{2,0,1:T(8,128)(2,1)} %copy-done.6) | copy-start | bytes 3538948
  78.6 2.0 %copy-start.15 = (f32[384,4]{0,1:T(4,128)S(1)}, f32[384,4]{0,1:T(4,128)}, u32[]{:S(2)}) copy-start(f32[384,4]{0,1:T(4,128)} %get-tuple-element.17) | copy-start | bytes 18436
  82.9 1.1 copy-start.12
  82.9 1.1 copy-start.18
  90.3 1.9 %copy-start.17 = (f32[384,4]{0,1:T(4,128)S(1)}, f32[384,4]{0,1:T(4,128)}, u32[]{:S(2)}) copy-start(f32[384,4]{0,1:T(4,128)} %get-tuple-element.19) | copy-start | bytes 18436
  102.5 35.8 %all-to-all-start.4 = ((bf16[384,16,128]{2,1,0:T(8,128)(2,1)}), bf16[384,16,128]{2,1,0:T(8,128)(2,1)}, u32[]{:S(2)}, u32[]{:S(2)}) async-start(bf16[384,16,128]{2,1,0:T(8,128)(2,1)} %copy.67), calls=%async_computation.4 | async-start | bytes 3145728 | tf_op jit(solution)/shard_map/all_to_all | solution.py:96
  107.2 6.7 %copy-start.2 = (f32[1152,1,128]{2,0,1:T(8,128)S(1)}, f32[1152,1,128]{2,0,1:T(8,128)}, u32[]{:S(2)}) copy-start(f32[1152,1,128]{2,0,1:T(8,128)} %fusion.25) | copy-start | bytes 1769476
  107.2 6.7 %copy-start.3 = (f32[1152,1,128]{2,0,1:T(8,128)S(1)}, f32[1152,1,128]{2,0,1:T(8,128)}, u32[]{:S(2)}) copy-start(f32[1152,1,128]{2,0,1:T(8,128)} %fusion.22) | copy-start | bytes 1769476
  107.2 6.7 %copy-start.4 = (f32[1152,1,128]{2,0,1:T(8,128)S(1)}, f32[1152,1,128]{2,0,1:T(8,128)}, u32[]{:S(2)}) copy-start(f32[1152,1,128]{2,0,1:T(8,128)} %fusion.19) | copy-start | bytes 1769476
  107.2 6.7 %copy-start.5 = (f32[1152,1,128]{2,0,1:T(8,128)S(1)}, f32[1152,1,128]{2,0,1:T(8,128)}, u32[]{:S(2)}) copy-start(f32[1152,1,128]{2,0,1:T(8,128)} %fusion.16) | copy-start | bytes 1769476
  108.8 22.6 %collective-permute-start.4 = (bf16[384,4,128]{2,0,1:T(8,128)(2,1)S(1)}, bf16[384,4,128]{2,0,1:T(8,128)(2,1)S(1)}, u32[]{:S(2)}, u32[]{:S(2)}) collective-permute-start(bf16[384,4,128]{2,0,1:T(8,128)(2,1)S(1)} %slice.219), channel_id=1, source_target_pairs={{2,0},{4,2},{6,4},{8,6},{10,8},{12,10},{14,12},{16,14},{18,16},{20... | collective-permute-start | bytes 1179656 | tf_op jit(solution)/shard_map/ppermute | solution.py:10
  114.1 21.6 %copy-start = (f32[1152,4,128]{2,0,1:T(8,128)}, f32[1152,4,128]{2,0,1:T(8,128)S(1)}, u32[]{:S(2)}) copy-start(f32[1152,4,128]{2,0,1:T(8,128)S(1)} %pad_maximum_fusion.1) | copy-start | bytes 7077892
  114.1 21.5 %collective-permute-start.6 = (bf16[384,4,128]{2,0,1:T(8,128)(2,1)S(1)}, bf16[384,4,128]{2,0,1:T(8,128)(2,1)S(1)}, u32[]{:S(2)}, u32[]{:S(2)}) collective-permute-start(bf16[384,4,128]{2,0,1:T(8,128)(2,1)S(1)} %slice.218), channel_id=1, source_target_pairs={{2,0},{4,2},{6,4},{8,6},{10,8},{12,10},{14,12},{16,14},{18,16},{20... | collective-permute-start | bytes 1179656 | tf_op jit(solution)/shard_map/ppermute | solution.py:10
  131.5 14.8 %collective-permute-start.5 = (bf16[384,4,128]{2,0,1:T(8,128)(2,1)S(1)}, bf16[384,4,128]{2,0,1:T(8,128)(2,1)S(1)}, u32[]{:S(2)}, u32[]{:S(2)}) collective-permute-start(bf16[384,4,128]{2,0,1:T(8,128)(2,1)S(1)} %fusion.36), channel_id=1, source_target_pairs={{2,0},{4,2},{6,4},{8,6},{10,8},{12,10},{14,12},{16,14},{18,16},{20... | collective-permute-start | bytes 1179656 | tf_op jit(solution)/shard_map/ppermute | solution.py:10
  136.4 15.0 %collective-permute-start.7 = (bf16[384,4,128]{2,0,1:T(8,128)(2,1)}, bf16[384,4,128]{2,0,1:T(8,128)(2,1)S(1)}, u32[]{:S(2)}, u32[]{:S(2)}) collective-permute-start(bf16[384,4,128]{2,0,1:T(8,128)(2,1)} %fusion.34), channel_id=1, source_target_pairs={{2,0},{4,2},{6,4},{8,6},{10,8},{12,10},{14,12},{16,14},{18,16},{20... | collective-permute-start | bytes 1179656 | tf_op jit(solution)/shard_map/ppermute | solution.py:10
  (2 other events, 2.1 us)
where the time goes:
time: 156 us; the launch traced here: 154 us
  waiting for transfers between devices  47.4 us (30%)
  starting transfers between devices  44.7 us (29%)
  matrix products  30.3 us (19%)
  local copies, waits for them, and re-layouts  22.7 us (15%)
  other arithmetic  7.53 us (5%)
    ppermute x8, waiting for transfers between devices, shifted(): return lax.ppermute(shard, axis, pairs)  28.4 us
    ppermute x8, starting transfers between devices, shifted(): return lax.ppermute(shard, axis, pairs)  24.6 us
    unnamed x52, local copies, waits for them, and re-layouts  12.8 us
    all_to_all x1, waiting for transfers between devices, body(): lax.all_to_all(output_gradient, 'head', split_axis=1, concat_axis=0, tile...  12.7 us
    dot_general x4, matrix products, body(): jnp.einsum('tgc,tgd->cd', prob_bf, grad_one, preferred_element_type=jnp.f...  7.66 us
    dot_general x4, matrix products, body(): jnp.einsum('tgd,cd->tgc', query_one, key_one, preferred_element_type=jnp....  7.44 us
    dot_general x4, matrix products, body(): jnp.einsum('tgc,tgd->cd', score_bf, query_one, preferred_element_type=jnp...  6.03 us
    all_to_all x1, starting transfers between devices, body(): lax.all_to_all(output_gradient, 'head', split_axis=1, concat_axis=0, tile...  4.79 us
  transfers between devices with their start and end apart: 13, of which 8 were waited for; matrix products, arithmetic and copies ran while one was open for 15% of the time, Pallas kernels for 0%

commit v1 on v0

v1 whole, which is shorter than its diff:
```python
import jax
import jax.numpy as jnp
from jax import lax
from jax.experimental import pallas as pl
from jax.experimental.pallas import tpu as pltpu
from jax.sharding import PartitionSpec as P

MESH = pl.DeviceIdType.MESH
BLK = 384
HALF = 192
WIN = 960
OWN_HEADS = 4
HEADS = 8
GROUP = 768
CHUNK = 256
SCALE = 128**-0.5
LOG2E = 1.4426950408889634

NT = (((1,), (1,)), ((), ()))
NN = (((1,), (0,)), ((), ()))
TN = (((0,), (0,)), ((), ()))


def dot(a, b, dims):
    return lax.dot_general(a, b, dims, preferred_element_type=jnp.float32)


def kernel(n_seq, kv_in, q_ref, do_ref, lse_ref, dl_ref, dq_ref, dk_ref, dv_ref,
           kvbuf, gacc, r3buf, r2buf, r1buf, dbuf, xbuf, ybuf,
           f1_s, f1_r, f2_s, f2_r, f3_s, f3_r, r1_s, r1_r, r2_s, r2_r, r3_s, r3_r):
    seq = lax.axis_index("seq")
    y = lax.axis_index("head")
    core = lax.rem(seq, 2)
    col = lax.rem(lax.div(seq, 2), 4)
    first_col = (col == 0).astype(jnp.int32)
    last_col = (col == 3).astype(jnp.int32)
    off = y * HALF
    nxt = (lax.rem(seq + 2, n_seq), jnp.where(last_col == 1, 1 - y, y))
    prv = (lax.rem(seq + n_seq - 2, n_seq), jnp.where(first_col == 1, 1 - y, y))
    pair = (seq + 1 - 2 * core, y)
    mate = (seq, 1 - y)

    def own(m):
        return 4 * y + m

    def other(m):
        return 4 * (1 - y) + m

    def stage_head(i):
        early = jnp.where(jnp.where(i < 2, 0, 1) == first_col, own(lax.rem(i, 2)), other(lax.rem(i, 2)))
        late = jnp.where(lax.rem(i, 2) == 1, own(lax.div(i, 2)), other(lax.div(i, 2)))
        return jnp.where(i < 4, early, late)

    def back_head(k):
        early = jnp.where(k < 2, own(lax.rem(k, 2)), other(lax.rem(k, 2)))
        late = jnp.where(lax.rem(k + last_col, 2) == 1, own(lax.div(k, 2)), other(lax.div(k, 2)))
        return jnp.where(k < 4, early, late)

    def rc(src, dst, s, r, dev):
        return pltpu.make_async_remote_copy(src_ref=src, dst_ref=dst, send_sem=s, recv_sem=r,
                                            device_id=dev, device_id_type=MESH)

    def slot(g, n):
        return kvbuf.at[g, :, pl.ds(n * BLK, BLK), :]

    def f1(m):
        g = own(m)
        return rc(kv_in.at[m], slot(g, 2), f1_s.at[m], f1_r.at[m], mate)

    def f2(src, g):
        return rc(src, slot(g, 0), f2_s.at[g], f2_r.at[g], nxt)

    def f3(src, g):
        return rc(src, slot(g, 1), f3_s.at[g], f3_r.at[g], pair)

    def r3(g):
        return rc(r3buf.at[g], dbuf.at[g], r3_s.at[g], r3_r.at[g], pair)

    def r2(g):
        return rc(r2buf.at[g], xbuf.at[g], r2_s.at[g], r2_r.at[g], prv)

    def r1(m):
        return rc(r1buf.at[m], ybuf.at[m], r1_s.at[m], r1_r.at[m], mate)

    barrier = pltpu.get_barrier_semaphore()
    for dev in (nxt, prv, pair, mate):
        pl.semaphore_signal(barrier, inc=1, device_id=dev, device_id_type=MESH)
    pl.semaphore_wait(barrier, 4)

    for m in range(OWN_HEADS):
        f1(m).start()
    f2(kv_in.at[0], own(0)).start()
    f2(kv_in.at[1], own(1)).start()

    @pl.when(core == 0)
    def _():
        for m in range(OWN_HEADS):
            f3(kv_in.at[m], own(m)).start()

    def keep(m, carry):
        kvbuf[own(m), :, pl.ds(2 * BLK, BLK), :] = kv_in[m]
        return carry

    lax.fori_loop(0, OWN_HEADS, keep, 0)

    tile0 = 2 * seq + y - 4

    def compute(g):
        k = kvbuf[g, 0, pl.ds(off, WIN), :]
        v = kvbuf[g, 1, pl.ds(off, WIN), :]
        dk = dv = None
        for c in range(GROUP // CHUNK):
            sl = slice(c * CHUNK, (c + 1) * CHUNK)
            q = q_ref[g, sl, :]
            do = do_ref[g, sl, :]
            lse = lse_ref[g, :, sl]
            st = dot(k, q, NT) * (SCALE * LOG2E)
            lane = lax.broadcasted_iota(jnp.int32, (HALF, CHUNK), 1) + c * CHUNK
            tok = lane - HALF * ((lane >= HALF).astype(jnp.int32) + (lane >= 2 * HALF).astype(jnp.int32)
                                 + (lane >= 3 * HALF).astype(jnp.int32))
            low = lax.broadcasted_iota(jnp.int32, (HALF, CHUNK), 0) > tok
            parts = []
            for n in range(5):
                shift = lse + jnp.where(tile0 + n < 0, 1e30, 0.0)
                part = jnp.exp2(st[n * HALF:(n + 1) * HALF] - shift)
                if n == 0:
                    part = jnp.where(low, part, 0.0)
                if n == 4:
                    part = jnp.where(low, 0.0, part)
                parts.append(part)
            p = jnp.concatenate(parts, 0)
            ds = (p * (dot(v, do, NT) - dl_ref[g, :, sl])).astype(jnp.bfloat16)
            dv_c = dot(p.astype(jnp.bfloat16), do, NN)
            dk_c = dot(ds, q, NN)
            dv = dv_c if dv is None else dv + dv_c
            dk = dk_c if dk is None else dk + dk_c
            dq_ref[g, sl, :] = (dot(ds, k, TN) * SCALE).astype(jnp.bfloat16)
        gacc[g, 0, pl.ds(off, WIN), :] = dk * SCALE
        gacc[g, 1, pl.ds(off, WIN), :] = dv
        gacc[g, :, pl.ds((1 - y) * WIN, HALF), :] = jnp.zeros((2, HALF, 128), jnp.float32)

    def stage(i, carry):
        @pl.when(i < OWN_HEADS)
        def _():
            g = other(i)
            f1(i).wait_recv()
            f2(slot(g, 2), g).start()

            @pl.when(core == 0)
            def _():
                f3(slot(g, 2), g).start()

            @pl.when(i >= 2)
            def _():
                f2(kv_in.at[i], own(i)).start()

        @pl.when((i >= 1) & (i < 9))
        def _():
            g = stage_head(i - 1)
            r3(g).wait_recv()

            @pl.when(core == 1)
            def _():
                r2buf[g] = (gacc[g, :, pl.ds(0, BLK), :] + dbuf[g].astype(jnp.float32)).astype(jnp.bfloat16)
                r2(g).start()

            @pl.when(core == 0)
            def _():
                gacc[g, :, pl.ds(2 * BLK, BLK), :] += dbuf[g].astype(jnp.float32)

        @pl.when(i >= 3)
        def _():
            g = back_head(i - 3)
            r2(g).wait_recv()
            total = gacc[g, :, pl.ds(2 * BLK, BLK), :] + xbuf[g].astype(jnp.float32)
            mine = lax.div(g, 4) == y

            @pl.when(mine)
            def _():
                gacc[g, :, pl.ds(2 * BLK, BLK), :] = total

            @pl.when(jnp.logical_not(mine))
            def _():
                m = lax.rem(g, 4)
                r1buf[m] = total.astype(jnp.bfloat16)
                r1(m).start()

        @pl.when(i < HEADS)
        def _():
            g = stage_head(i)
            f2(slot(g, 2), g).wait_recv()

            @pl.when(core == 1)
            def _():
                f3(slot(g, 0), g).start()

            f3(slot(g, 0), g).wait_recv()
            compute(g)
            r3buf[g] = gacc[g, :, pl.ds(BLK, BLK), :].astype(jnp.bfloat16)

            @pl.when(core == 0)
            def _():
                r2buf[g] = gacc[g, :, pl.ds(0, BLK), :].astype(jnp.bfloat16)
                r2(g).start()

            r3(g).start()

        return carry

    lax.fori_loop(0, HEADS + 3, stage, 0)

    def finish(m, carry):
        r1(m).wait_recv()
        g = own(m)
        dk_ref[m] = (gacc[g, 0, pl.ds(2 * BLK, BLK), :] + ybuf[m, 0].astype(jnp.float32)).astype(jnp.bfloat16)
        dv_ref[m] = (gacc[g, 1, pl.ds(2 * BLK, BLK), :] + ybuf[m, 1].astype(jnp.float32)).astype(jnp.bfloat16)
        f1(m).wait_send()
        r1(m).wait_send()
        return carry

    lax.fori_loop(0, OWN_HEADS, finish, 0)

    def drain(g, carry):
        f2(slot(g, 2), g).wait_send()
        f3(slot(g, 2), g).wait_send()
        r2(g).wait_send()
        r3(g).wait_send()
        return carry

    lax.fori_loop(0, HEADS, drain, 0)


def attention_grads(n_seq, kv, q, do, lse, delta):
    vm = pl.BlockSpec(memory_space=pltpu.VMEM)
    bf, f32 = jnp.bfloat16, jnp.float32
    dma = pltpu.SemaphoreType.DMA
    return pl.pallas_call(
        lambda *refs: kernel(n_seq, *refs),
        out_shape=(
            jax.ShapeDtypeStruct((HEADS, GROUP, 128), bf),
            jax.ShapeDtypeStruct((OWN_HEADS, BLK, 128), bf),
            jax.ShapeDtypeStruct((OWN_HEADS, BLK, 128), bf),
        ),
        in_specs=[vm] * 5,
        out_specs=(vm, vm, vm),
        scratch_shapes=[
            pltpu.VMEM((HEADS, 2, 3 * BLK, 128), bf),
            pltpu.VMEM((HEADS, 2, 3 * BLK, 128), f32),
            pltpu.VMEM((HEADS, 2, BLK, 128), bf),
            pltpu.VMEM((HEADS, 2, BLK, 128), bf),
            pltpu.VMEM((OWN_HEADS, 2, BLK, 128), bf),
            pltpu.VMEM((HEADS, 2, BLK, 128), bf),
            pltpu.VMEM((HEADS, 2, BLK, 128), bf),
            pltpu.VMEM((OWN_HEADS, 2, BLK, 128), bf),
            dma((4,)), dma((4,)), dma((8,)), dma((8,)), dma((8,)), dma((8,)),
            dma((4,)), dma((4,)), dma((8,)), dma((8,)), dma((8,)), dma((8,)),
        ],
        compiler_params=pltpu.CompilerParams(
            collective_id=0, has_side_effects=True, vmem_limit_bytes=52 * 2**20
        ),
        name="window_grads",
    )(kv, q, do, lse, delta)


def body(n_seq, queries, keys, values, outputs, output_gradient, lse):
    delta = jnp.sum(output_gradient.astype(jnp.float32) * outputs.astype(jnp.float32), axis=-1)
    rows = lambda a: a.transpose(1, 0).reshape(HEADS, 1, GROUP)
    major = lambda a: a.transpose(1, 0, 2)
    kv = jnp.stack([major(keys), major(values)], 1)
    dq, dk, dv = attention_grads(
        n_seq, kv, major(queries).reshape(HEADS, GROUP, 128), major(output_gradient).reshape(HEADS, GROUP, 128),
        rows(lse) * LOG2E, rows(delta),
    )
    return major(dq.reshape(4 * HEADS, HALF, 128)), major(dk), major(dv)


def solution(mesh):
    n_seq = mesh.shape["seq"]
    return jax.shard_map(
        lambda *args: body(n_seq, *args),
        mesh=mesh,
        in_specs=(
            P(("seq", "head"), None, None),
            P("seq", "head", None),
            P("seq", "head", None),
            P(("seq", "head"), None, None),
            P(("seq", "head"), None, None),
            P(("seq", "head"), None),
        ),
        out_specs=(P(("seq", "head"), None, None), P("seq", "head", None), P("seq", "head", None)),
        check_vma=False,
    )
```

time: 156 us -> 85 us (0.54); the launches traced: 154 us -> 84.8 us
  Pallas kernels: 0 us -> 69.6 us
  waiting for transfers between devices: 47.4 us -> 0 us
  starting transfers between devices: 44.7 us -> 0 us
  matrix products: 30.3 us -> 0 us
  local copies, waits for them, and re-layouts: 22.7 us -> 10.8 us
  other arithmetic: 7.53 us -> 3.68 us
    pallas_call x0 -> x1, Pallas kernels: none -> 69.6 us  [attention_grads(): pl.pallas_call(lambda *refs: kernel(n_seq, *refs), out_shape=(jax.ShapeDt...]
    dot_general x20 -> x0, matrix products: 30.3 us -> none  [the longest x4 7.66 us: body(): jnp.einsum('tgc,tgd->cd', prob_bf, grad_one, preferred_element_type=jnp.f...]
    ppermute x8 -> x0, waiting for transfers between devices: 28.4 us -> none  [shifted(): return lax.ppermute(shard, axis, pairs)]
    ppermute x8 -> x0, starting transfers between devices: 24.6 us -> none  [shifted(): return lax.ppermute(shard, axis, pairs)]
    all_to_all x5 -> x0, starting transfers between devices: 20.1 us -> none  [the longest x1 4.79 us: body(): lax.all_to_all(output_gradient, 'head', split_axis=1, concat_axis=0, tile...]
    all_to_all x5 -> x0, waiting for transfers between devices: 18.9 us -> none  [the longest x1 12.7 us: body(): lax.all_to_all(output_gradient, 'head', split_axis=1, concat_axis=0, tile...]
    unnamed x52 -> x10, local copies, waits for them, and re-layouts: 12.8 us -> 3.33 us
    all_to_all x5 -> x0, local copies, waits for them, and re-layouts: 4.62 us -> none  [the longest x1 2.82 us: body(): lax.all_to_all(query_local, 'head', split_axis=0, concat_axis=1, tiled=True)]
  transfers between devices with their start and end apart: 13 -> 0, of which waited for: 8 -> 0; matrix products, arithmetic and copies ran while one was open for 15% -> 0% of each run, Pallas kernels for 0% -> 0%
where the time goes in v1:
time: 85 us; the launch traced here: 84.8 us
  Pallas kernels  69.6 us (82%)
  local copies, waits for them, and re-layouts  10.8 us (13%)
  other arithmetic  3.68 us (4%)
    pallas_call x1, Pallas kernels, attention_grads(): pl.pallas_call(lambda *refs: kernel(n_seq, *refs), out_shape=(jax.ShapeDt...  69.6 us
    reshape x1, local copies, waits for them, and re-layouts, body(): return (major(dq.reshape(4 * HEADS, HALF, 128)), major(dk), major(dv))  3.57 us
    transpose x2, local copies, waits for them, and re-layouts, body(): major = lambda a: a.transpose(1, 0, 2)  3.53 us
    unnamed x10, local copies, waits for them, and re-layouts  3.33 us
    reduce_sum x1, other arithmetic, body(): jnp.sum(output_gradient.astype(jnp.float32) * outputs.astype(jnp.float32)...  2.84 us

profile of v1, /device:TPU:119, one launch (start us, length us, event | category | flops | bytes accessed | tf_op | source)
XLA Modules:
  0.0 84.8 jit_solution(9168075543805392634)
XLA Ops:
  0.6 0.8 multiply_bitcast_fusion
  1.4 0.1 mul.16.refs_3_
  1.5 0.0 copy-start.2
  1.5 0.0 copy-start.3
  1.5 2.8 %multiply_reduce_fusion = f32[192,32]{1,0:T(8,128)S(1)} fusion(bf16[192,32,128]{2,1,0:T(8,128)(2,1)} %param.9, bf16[192,32,128]{2,1,0:T(8,128)(2,1)} %param.10), kind=kLoop, calls=%fused_computation | loop fusion | flops 3139584 | bytes 3170304 | tf_op jit(solution)/shard_map/reduce_sum | solution.py:266
  4.4 0.1 copy.20
  4.4 0.1 reshape.35.refs_4_
  4.5 0.0 copy-done.2
  4.5 0.0 copy-done.3
  4.5 0.0 copy-start.1
  4.6 0.1 copy_bitcast_fusion.1
  4.7 0.1 pad_maximum_fusion.refs_0_
  4.8 1.2 %copy-done.1 = bf16[192,32,128]{2,1,0:T(8,128)(2,1)S(1)} copy-done((bf16[192,32,128]{2,1,0:T(8,128)(2,1)S(1)}, bf16[192,32,128]{2,1,0:T(8,128)(2,1)}, u32[]{:S(2)}) %copy-start.1) | copy-done | bytes 1572888
  6.0 0.0 copy-start
  6.0 1.8 %copy.18 = bf16[32,192,128]{2,1,0:T(8,128)(2,1)} copy(bf16[32,192,128]{2,0,1:T(8,128)(2,1)S(1)} %bitcast.26) | data formatting | bytes 3145728 | tf_op jit(solution)/shard_map/transpose | solution.py:268
  7.7 0.0 copy-done
  7.7 1.8 %copy.19 = bf16[32,192,128]{2,1,0:T(8,128)(2,1)} copy(bf16[32,192,128]{2,0,1:T(8,128)(2,1)S(1)} %bitcast.23) | data formatting | bytes 3145728 | tf_op jit(solution)/shard_map/transpose | solution.py:268
  9.5 69.6 %window_grads.1 = (bf16[8,768,128]{2,1,0:T(8,128)(2,1)}, bf16[4,384,128]{2,1,0:T(8,128)(2,1)S(1)}, bf16[4,384,128]{2,1,0:T(8,128)(2,1)S(1)}) custom-call(bf16[4,2,384,128]{3,2,1,0:T(8,128)(2,1)S(1)} %pad_maximum_fusion.refs_0_, bf16[8,768,128]{2,1,0:T(8,128)(2,1)} %bitcast.24, bf16[8,768,128]{2,1,0:T(8,128)(2,1)} %bitcast.25, f32[8,1,768]{2,1,0:T(1,128)S(1)} %mul.16.refs_3_, ...), custom_call_target="tpu_custom_call" | custom-call | tf_op jit(solution)/shard_map/window_grads/pallas_call | solution.py:237
  79.1 3.6 %copy.27 = bf16[32,192,128]{2,0,1:T(8,128)(2,1)} copy(bf16[32,192,128]{2,1,0:T(8,128)(2,1)} %bitcast.28) | data formatting | bytes 3145728 | tf_op jit(solution)/shard_map/reshape | solution.py:274
  82.7 1.1 %copy.22 = bf16[384,4,128]{2,1,0:T(4,128)(2,1)} copy(bf16[384,4,128]{2,0,1:T(8,128)(2,1)S(1)} %bitcast.22) | data formatting | bytes 786432
  83.7 1.1 %copy.23 = bf16[384,4,128]{2,1,0:T(4,128)(2,1)} copy(bf16[384,4,128]{2,0,1:T(8,128)(2,1)S(1)} %bitcast.21) | data formatting | bytes 786432
Async XLA Ops:
  1.5 3.0 %copy-start.2 = (bf16[384,4,128]{2,1,0:T(4,128)(2,1)S(1)}, bf16[384,4,128]{2,1,0:T(4,128)(2,1)}, u32[]{:S(2)}) copy-start(bf16[384,4,128]{2,1,0:T(4,128)(2,1)} %param.8) | copy-start | bytes 1179652
  1.5 3.0 %copy-start.3 = (bf16[384,4,128]{2,1,0:T(4,128)(2,1)S(1)}, bf16[384,4,128]{2,1,0:T(4,128)(2,1)}, u32[]{:S(2)}) copy-start(bf16[384,4,128]{2,1,0:T(4,128)(2,1)} %param.7) | copy-start | bytes 1179652
  4.5 1.4 %copy-start.1 = (bf16[192,32,128]{2,1,0:T(8,128)(2,1)S(1)}, bf16[192,32,128]{2,1,0:T(8,128)(2,1)}, u32[]{:S(2)}) copy-start(bf16[192,32,128]{2,1,0:T(8,128)(2,1)} %param.6) | copy-start | bytes 4718596
  6.0 1.8 %copy-start = (bf16[192,32,128]{2,1,0:T(8,128)(2,1)S(1)}, bf16[192,32,128]{2,1,0:T(8,128)(2,1)}, u32[]{:S(2)}) copy-start(bf16[192,32,128]{2,1,0:T(8,128)(2,1)} %param.10) | copy-start | bytes 4718596

commit v2 on v1

--- a/solution.py
+++ b/solution.py
@@ -13,6 +13,7 @@
 HEADS = 8
 GROUP = 768
 CHUNK = 256
+LAG = 3
 SCALE = 128**-0.5
 LOG2E = 1.4426950408889634
 
@@ -25,8 +26,8 @@
     return lax.dot_general(a, b, dims, preferred_element_type=jnp.float32)
 
 
-def kernel(n_seq, kv_in, q_ref, do_ref, lse_ref, dl_ref, dq_ref, dk_ref, dv_ref,
-           kvbuf, gacc, r3buf, r2buf, r1buf, dbuf, xbuf, ybuf,
+def kernel(n_seq, k_hbm, v_hbm, q_hbm, do_hbm, o_hbm, lse_hbm, dq_out, dk_ref, dv_ref,
+           raw, raw_k, raw_v, lse_in, in_s, kv_in, kv_out, q_ref, do_ref, o_ref, lse_ref, dq_ref, kvbuf, gacc, r3buf, r2buf, r1buf, dbuf, xbuf, ybuf,
            f1_s, f1_r, f2_s, f2_r, f3_s, f3_r, r1_s, r1_r, r2_s, r2_r, r3_s, r3_r):
     seq = lax.axis_index("seq")
     y = lax.axis_index("head")
@@ -35,6 +36,8 @@
     first_col = (col == 0).astype(jnp.int32)
     last_col = (col == 3).astype(jnp.int32)
     off = y * HALF
+    starts = seq < 2
+    ends = seq >= n_seq - 2
     nxt = (lax.rem(seq + 2, n_seq), jnp.where(last_col == 1, 1 - y, y))
     prv = (lax.rem(seq + n_seq - 2, n_seq), jnp.where(first_col == 1, 1 - y, y))
     pair = (seq + 1 - 2 * core, y)
@@ -48,12 +51,12 @@
 
     def stage_head(i):
         early = jnp.where(jnp.where(i < 2, 0, 1) == first_col, own(lax.rem(i, 2)), other(lax.rem(i, 2)))
-        late = jnp.where(lax.rem(i, 2) == 1, own(lax.div(i, 2)), other(lax.div(i, 2)))
+        late = jnp.where(jnp.where(i < 6, 1, 0) == first_col, own(2 + lax.rem(i, 2)), other(2 + lax.rem(i, 2)))
         return jnp.where(i < 4, early, late)
 
     def back_head(k):
         early = jnp.where(k < 2, own(lax.rem(k, 2)), other(lax.rem(k, 2)))
-        late = jnp.where(lax.rem(k + last_col, 2) == 1, own(lax.div(k, 2)), other(lax.div(k, 2)))
+        late = jnp.where(k < 6, other(2 + lax.rem(k, 2)), own(2 + lax.rem(k, 2)))
         return jnp.where(k < 4, early, late)
 
     def rc(src, dst, s, r, dev):
@@ -82,15 +85,31 @@
     def r1(m):
         return rc(r1buf.at[m], ybuf.at[m], r1_s.at[m], r1_r.at[m], mate)
 
+    loads = [pltpu.make_async_copy(src, dst, in_s.at[n]) for n, (src, dst) in enumerate((
+        (q_hbm, raw.at[0]), (do_hbm, raw.at[1]), (o_hbm, raw.at[2]), (k_hbm, raw_k), (v_hbm, raw_v), (lse_hbm, lse_in)))]
+    for load in loads[3:5] + loads[:3] + loads[5:]:
+        load.start()
     barrier = pltpu.get_barrier_semaphore()
-    for dev in (nxt, prv, pair, mate):
-        pl.semaphore_signal(barrier, inc=1, device_id=dev, device_id_type=MESH)
-    pl.semaphore_wait(barrier, 4)
+    for dev, skip in ((nxt, ends), (prv, starts), (pair, None), (mate, None)):
+        def greet(dev=dev):
+            pl.semaphore_signal(barrier, inc=1, device_id=dev, device_id_type=MESH)
+
+        if skip is None:
+            greet()
+        else:
+            pl.when(jnp.logical_not(skip))(greet)
+    for n, src in enumerate((raw_k, raw_v)):
+        loads[3 + n].wait()
+        kv_in[:, n] = jnp.transpose(src[...], (1, 0, 2))
+    pl.semaphore_wait(barrier, jnp.where(starts | ends, 3, 4))
 
     for m in range(OWN_HEADS):
         f1(m).start()
-    f2(kv_in.at[0], own(0)).start()
-    f2(kv_in.at[1], own(1)).start()
+
+    @pl.when(jnp.logical_not(ends))
+    def _():
+        f2(kv_in.at[0], own(0)).start()
+        f2(kv_in.at[1], own(1)).start()
 
     @pl.when(core == 0)
     def _():
@@ -102,6 +121,21 @@
         return carry
 
     lax.fori_loop(0, OWN_HEADS, keep, 0)
+
+    @pl.when(starts)
+    def _():
+        def clear(g, carry):
+            kvbuf[g, :, pl.ds(0, BLK), :] = jnp.zeros((2, BLK, 128), jnp.bfloat16)
+            return carry
+
+        lax.fori_loop(0, HEADS, clear, 0)
+
+    for n, dst in enumerate((q_ref, do_ref, o_ref)):
+        loads[n].wait()
+        dst[...] = jnp.transpose(raw[n], (1, 0, 2)).reshape(HEADS, GROUP, 128)
+    loads[5].wait()
+    for h in range(4 * HEADS):
+        lse_ref[h // 4, :, h % 4 * HALF:(h % 4 + 1) * HALF] = lse_in[h:h + 1, :] * LOG2E
 
     tile0 = 2 * seq + y - 4
 
@@ -129,7 +163,12 @@
                     part = jnp.where(low, 0.0, part)
                 parts.append(part)
             p = jnp.concatenate(parts, 0)
-            ds = (p * (dot(v, do, NT) - dl_ref[g, :, sl])).astype(jnp.bfloat16)
+            prod = do.astype(jnp.float32) * o_ref[g, sl, :].astype(jnp.float32)
+            high = prod.astype(jnp.bfloat16)
+            rest = (prod - high.astype(jnp.float32)).astype(jnp.bfloat16)
+            ones = jnp.ones((16, 128), jnp.bfloat16)
+            delta = (dot(ones, high, NT) + dot(ones, rest, NT))[:1]
+            ds = (p * (dot(v, do, NT) - delta)).astype(jnp.bfloat16)
             dv_c = dot(p.astype(jnp.bfloat16), do, NN)
             dk_c = dot(ds, q, NN)
             dv = dv_c if dv is None else dv + dv_c
@@ -144,22 +183,38 @@
         def _():
             g = other(i)
             f1(i).wait_recv()
-            f2(slot(g, 2), g).start()
+
+            @pl.when(jnp.logical_not(ends))
+            def _():
+                f2(slot(g, 2), g).start()
+
+                @pl.when(i == 3)
+                def _():
+                    f2(kv_in.at[2], own(2)).start()
+                    f2(kv_in.at[3], own(3)).start()
 
             @pl.when(core == 0)
             def _():
                 f3(slot(g, 2), g).start()
 
-            @pl.when(i >= 2)
-            def _():
-                f2(kv_in.at[i], own(i)).start()
+        @pl.when(i < HEADS)
+        def _():
+            g = stage_head(i)
+
+            @pl.when(jnp.logical_not(starts))
+            def _():
+                f2(slot(g, 2), g).wait_recv()
+
+            @pl.when(core == 1)
+            def _():
+                f3(slot(g, 0), g).start()
 
         @pl.when((i >= 1) & (i < 9))
         def _():
             g = stage_head(i - 1)
             r3(g).wait_recv()
 
-            @pl.when(core == 1)
+            @pl.when((core == 1) & jnp.logical_not(starts))
             def _():
                 r2buf[g] = (gacc[g, :, pl.ds(0, BLK), :] + dbuf[g].astype(jnp.float32)).astype(jnp.bfloat16)
                 r2(g).start()
@@ -168,52 +223,47 @@
             def _():
                 gacc[g, :, pl.ds(2 * BLK, BLK), :] += dbuf[g].astype(jnp.float32)
 
-        @pl.when(i >= 3)
-        def _():
-            g = back_head(i - 3)
-            r2(g).wait_recv()
-            total = gacc[g, :, pl.ds(2 * BLK, BLK), :] + xbuf[g].astype(jnp.float32)
-            mine = lax.div(g, 4) == y
-
-            @pl.when(mine)
-            def _():
-                gacc[g, :, pl.ds(2 * BLK, BLK), :] = total
-
-            @pl.when(jnp.logical_not(mine))
+        @pl.when(i >= LAG)
+        def _():
+            g = back_head(i - LAG)
+
+            @pl.when(jnp.logical_not(ends))
+            def _():
+                r2(g).wait_recv()
+                gacc[g, :, pl.ds(2 * BLK, BLK), :] += xbuf[g].astype(jnp.float32)
+
+            @pl.when(lax.div(g, 4) != y)
             def _():
                 m = lax.rem(g, 4)
-                r1buf[m] = total.astype(jnp.bfloat16)
+                r1buf[m] = gacc[g, :, pl.ds(2 * BLK, BLK), :].astype(jnp.bfloat16)
                 r1(m).start()
 
         @pl.when(i < HEADS)
         def _():
             g = stage_head(i)
-            f2(slot(g, 2), g).wait_recv()
-
-            @pl.when(core == 1)
-            def _():
-                f3(slot(g, 0), g).start()
-
             f3(slot(g, 0), g).wait_recv()
             compute(g)
             r3buf[g] = gacc[g, :, pl.ds(BLK, BLK), :].astype(jnp.bfloat16)
 
-            @pl.when(core == 0)
+            @pl.when((core == 0) & jnp.logical_not(starts))
             def _():
                 r2buf[g] = gacc[g, :, pl.ds(0, BLK), :].astype(jnp.bfloat16)
                 r2(g).start()
 
             r3(g).start()
 
+        @pl.when(i == HEADS)
+        def _():
+            dq_out[...] = jnp.transpose(dq_ref[...].reshape(4 * HEADS, HALF, 128), (1, 0, 2))
+
         return carry
 
-    lax.fori_loop(0, HEADS + 3, stage, 0)
+    lax.fori_loop(0, HEADS + LAG, stage, 0)
 
     def finish(m, carry):
         r1(m).wait_recv()
         g = own(m)
-        dk_ref[m] = (gacc[g, 0, pl.ds(2 * BLK, BLK), :] + ybuf[m, 0].astype(jnp.float32)).astype(jnp.bfloat16)
-        dv_ref[m] = (gacc[g, 1, pl.ds(2 * BLK, BLK), :] + ybuf[m, 1].astype(jnp.float32)).astype(jnp.bfloat16)
+        kv_out[m] = (gacc[g, :, pl.ds(2 * BLK, BLK), :] + ybuf[m].astype(jnp.float32)).astype(jnp.bfloat16)
         f1(m).wait_send()
         r1(m).wait_send()
         return carry
@@ -221,29 +271,59 @@
     lax.fori_loop(0, OWN_HEADS, finish, 0)
 
     def drain(g, carry):
-        f2(slot(g, 2), g).wait_send()
+        @pl.when(jnp.logical_not(ends))
+        def _():
+            f2(slot(g, 2), g).wait_send()
+
+        @pl.when(jnp.logical_not(starts))
+        def _():
+            r2(g).wait_send()
+
         f3(slot(g, 2), g).wait_send()
-        r2(g).wait_send()
         r3(g).wait_send()
         return carry
 
     lax.fori_loop(0, HEADS, drain, 0)
-
-
-def attention_grads(n_seq, kv, q, do, lse, delta):
-    vm = pl.BlockSpec(memory_space=pltpu.VMEM)
+    dk_ref[...] = jnp.transpose(kv_out[:, 0], (1, 0, 2))
+    dv_ref[...] = jnp.transpose(kv_out[:, 1], (1, 0, 2))
+
+
+def store(a_ref, b_ref, c_ref, a_out, b_out, c_out, sem):
+    copies = [pltpu.make_async_copy(src, dst, sem.at[n])
+              for n, (src, dst) in enumerate(((a_ref, a_out), (b_ref, b_out), (c_ref, c_out)))]
+    for copy in copies:
+        copy.start()
+    for copy in copies:
+        copy.wait()
+
+
+def attention_grads(n_seq, k, v, q, do, o, lse):
+    vm, hbm = pl.BlockSpec(memory_space=pltpu.VMEM), pl.BlockSpec(memory_space=pltpu.HBM)
     bf, f32 = jnp.bfloat16, jnp.float32
     dma = pltpu.SemaphoreType.DMA
-    return pl.pallas_call(
+    shapes = (
+        jax.ShapeDtypeStruct((HALF, 4 * HEADS, 128), bf),
+        jax.ShapeDtypeStruct((BLK, OWN_HEADS, 128), bf),
+        jax.ShapeDtypeStruct((BLK, OWN_HEADS, 128), bf),
+    )
+    grads = pl.pallas_call(
         lambda *refs: kernel(n_seq, *refs),
-        out_shape=(
-            jax.ShapeDtypeStruct((HEADS, GROUP, 128), bf),
-            jax.ShapeDtypeStruct((OWN_HEADS, BLK, 128), bf),
-            jax.ShapeDtypeStruct((OWN_HEADS, BLK, 128), bf),
-        ),
-        in_specs=[vm] * 5,
+        out_shape=shapes,
+        in_specs=[hbm] * 6,
         out_specs=(vm, vm, vm),
         scratch_shapes=[
+            pltpu.VMEM((3, HALF, 4 * HEADS, 128), bf),
+            pltpu.VMEM((BLK, OWN_HEADS, 128), bf),
+            pltpu.VMEM((BLK, OWN_HEADS, 128), bf),
+            pltpu.VMEM((4 * HEADS, HALF), f32),
+            dma((6,)),
+            pltpu.VMEM((OWN_HEADS, 2, BLK, 128), bf),
+            pltpu.VMEM((OWN_HEADS, 2, BLK, 128), bf),
+            pltpu.VMEM((HEADS, GROUP, 128), bf),
+            pltpu.VMEM((HEADS, GROUP, 128), bf),
+            pltpu.VMEM((HEADS, GROUP, 128), bf),
+            pltpu.VMEM((HEADS, 1, GROUP), f32),
+            pltpu.VMEM((HEADS, GROUP, 128), bf),
             pltpu.VMEM((HEADS, 2, 3 * BLK, 128), bf),
             pltpu.VMEM((HEADS, 2, 3 * BLK, 128), f32),
             pltpu.VMEM((HEADS, 2, BLK, 128), bf),
@@ -256,22 +336,23 @@
             dma((4,)), dma((4,)), dma((8,)), dma((8,)), dma((8,)), dma((8,)),
         ],
         compiler_params=pltpu.CompilerParams(
-            collective_id=0, has_side_effects=True, vmem_limit_bytes=52 * 2**20
+            collective_id=0, has_side_effects=True, vmem_limit_bytes=50 * 2**20
         ),
         name="window_grads",
-    )(kv, q, do, lse, delta)
+    )(*(pltpu.with_memory_space_constraint(a, pltpu.HBM) for a in (k, v, q, do, o, lse)))
+    return pl.pallas_call(
+        store,
+        out_shape=shapes,
+        in_specs=[vm] * 3,
+        out_specs=(hbm, hbm, hbm),
+        scratch_shapes=[dma((3,))],
+        compiler_params=pltpu.CompilerParams(vmem_limit_bytes=8 * 2**20),
+        name="store_grads",
+    )(*grads)
 
 
 def body(n_seq, queries, keys, values, outputs, output_gradient, lse):
-    delta = jnp.sum(output_gradient.astype(jnp.float32) * outputs.astype(jnp.float32), axis=-1)
-    rows = lambda a: a.transpose(1, 0).reshape(HEADS, 1, GROUP)
-    major = lambda a: a.transpose(1, 0, 2)
-    kv = jnp.stack([major(keys), major(values)], 1)
-    dq, dk, dv = attention_grads(
-        n_seq, kv, major(queries).reshape(HEADS, GROUP, 128), major(output_gradient).reshape(HEADS, GROUP, 128),
-        rows(lse) * LOG2E, rows(delta),
-    )
-    return major(dq.reshape(4 * HEADS, HALF, 128)), major(dk), major(dv)
+    return attention_grads(n_seq, keys, values, queries, output_gradient, outputs, lse.transpose(1, 0))
 
 
 def solution(mesh):

time: 85 us -> 57.2 us (0.67); the launches traced: 84.8 us -> 56.1 us
  Pallas kernels: 69.6 us -> 55.5 us
  local copies, waits for them, and re-layouts: 10.8 us -> 0 us
  other arithmetic: 3.68 us -> 0 us
    pallas_call x1 -> x2, Pallas kernels: 69.6 us -> 55.5 us  [the longest x1 54 us: attention_grads(): pl.pallas_call(lambda *refs: kernel(n_seq, *refs), out_shape=shapes, in_s...]
    reshape x2 -> x0, local copies, waits for them, and re-layouts: 3.67 us -> none  [the longest x1 3.57 us: body(): return (major(dq.reshape(4 * HEADS, HALF, 128)), major(dk), major(dv))]
    transpose x3 -> x0, local copies, waits for them, and re-layouts: 3.59 us -> none  [the longest x2 3.53 us: body(): major = lambda a: a.transpose(1, 0, 2)]
    unnamed x10 -> x0, local copies, waits for them, and re-layouts: 3.33 us -> none
    reduce_sum x1 -> x0, other arithmetic: 2.84 us -> none  [body(): jnp.sum(output_gradient.astype(jnp.float32) * outputs.astype(jnp.float32)...]
where the time goes in v2:
time: 57.2 us; the launch traced here: 56.1 us
  Pallas kernels  55.5 us (97%)
  between operations  0.64 us (1%)
    pallas_call x1, Pallas kernels, attention_grads(): pl.pallas_call(lambda *refs: kernel(n_seq, *refs), out_shape=shapes, in_s...  54 us
    pallas_call x1, Pallas kernels, attention_grads(): pl.pallas_call(store, out_shape=shapes, in_specs=[vm] * 3, out_specs=(hbm...  1.42 us

profile of v2, /device:TPU:119, one launch (start us, length us, event | category | flops | bytes accessed | tf_op | source)
XLA Modules:
  0.0 56.1 jit_solution(1782257026969525517)
XLA Ops:
  0.6 54.0 %window_grads.1 = (bf16[192,32,128]{2,1,0:T(8,128)(2,1)S(1)}, bf16[384,4,128]{2,1,0:T(4,128)(2,1)S(1)}, bf16[384,4,128]{2,1,0:T(4,128)(2,1)S(1)}) custom-call(bf16[384,4,128]{2,1,0:T(4,128)(2,1)} %refs_0_.1, bf16[384,4,128]{2,1,0:T(4,128)(2,1)} %refs_1_.1, bf16[192,32,128]{2,1,0:T(8,128)(2,1)} %refs_2_.1, bf16[192,32,128]{2,1,0:T(8,128)(2,1)} %refs_3_.1, ...), custom_call_target="tpu_custom_call" | custom-call | tf_op jit(solution)/shard_map/window_grads/pallas_call | solution.py:309
  54.7 1.4 %store_grads.1 = (bf16[192,32,128]{2,1,0:T(8,128)(2,1)}, bf16[384,4,128]{2,1,0:T(4,128)(2,1)}, bf16[384,4,128]{2,1,0:T(4,128)(2,1)}) custom-call(bf16[192,32,128]{2,1,0:T(8,128)(2,1)S(1)} %get-tuple-element.6.a_ref, bf16[384,4,128]{2,1,0:T(4,128)(2,1)S(1)} %get-tuple-element.7.b_ref, bf16[384,4,128]{2,1,0:T(4,128)(2,1)S(1)} %get-tuple-element.8.c_ref), custom_call_target="tpu_custom_call" | custom-call | tf_op jit(solution)/shard_map/store_grads/pallas_call | solution.py:343

commit v3 on v2

--- a/solution.py
+++ b/solution.py
@@ -27,7 +27,7 @@
 
 
 def kernel(n_seq, k_hbm, v_hbm, q_hbm, do_hbm, o_hbm, lse_hbm, dq_out, dk_ref, dv_ref,
-           raw, raw_k, raw_v, lse_in, in_s, kv_in, kv_out, q_ref, do_ref, o_ref, lse_ref, dq_ref, kvbuf, gacc, r3buf, r2buf, r1buf, dbuf, xbuf, ybuf,
+           raw, raw_k, raw_v, lse_in, in_s, kv_in, kv_out, q_ref, do_ref, o_ref, lse_ref, dl_ref, dq_ref, kvbuf, gacc, r3buf, r2buf, r1buf, dbuf, xbuf, ybuf,
            f1_s, f1_r, f2_s, f2_r, f3_s, f3_r, r1_s, r1_r, r2_s, r2_r, r3_s, r3_r):
     seq = lax.axis_index("seq")
     y = lax.axis_index("head")
@@ -137,6 +137,16 @@
     for h in range(4 * HEADS):
         lse_ref[h // 4, :, h % 4 * HALF:(h % 4 + 1) * HALF] = lse_in[h:h + 1, :] * LOG2E
 
+    def row_sums(g, carry):
+        prod = do_ref[g].astype(jnp.float32) * o_ref[g].astype(jnp.float32)
+        high = prod.astype(jnp.bfloat16)
+        rest = (prod - high.astype(jnp.float32)).astype(jnp.bfloat16)
+        ones = jnp.ones((16, 128), jnp.bfloat16)
+        dl_ref[g] = (dot(ones, high, NT) + dot(ones, rest, NT))[:1]
+        gacc[g, :, pl.ds((1 - y) * WIN, HALF), :] = jnp.zeros((2, HALF, 128), jnp.float32)
+        return carry
+
+    lax.fori_loop(0, HEADS, row_sums, 0)
     tile0 = 2 * seq + y - 4
 
     def compute(g):
@@ -163,12 +173,7 @@
                     part = jnp.where(low, 0.0, part)
                 parts.append(part)
             p = jnp.concatenate(parts, 0)
-            prod = do.astype(jnp.float32) * o_ref[g, sl, :].astype(jnp.float32)
-            high = prod.astype(jnp.bfloat16)
-            rest = (prod - high.astype(jnp.float32)).astype(jnp.bfloat16)
-            ones = jnp.ones((16, 128), jnp.bfloat16)
-            delta = (dot(ones, high, NT) + dot(ones, rest, NT))[:1]
-            ds = (p * (dot(v, do, NT) - delta)).astype(jnp.bfloat16)
+            ds = (p * (dot(v, do, NT) - dl_ref[g, :, sl])).astype(jnp.bfloat16)
             dv_c = dot(p.astype(jnp.bfloat16), do, NN)
             dk_c = dot(ds, q, NN)
             dv = dv_c if dv is None else dv + dv_c
@@ -176,7 +181,20 @@
             dq_ref[g, sl, :] = (dot(ds, k, TN) * SCALE).astype(jnp.bfloat16)
         gacc[g, 0, pl.ds(off, WIN), :] = dk * SCALE
         gacc[g, 1, pl.ds(off, WIN), :] = dv
-        gacc[g, :, pl.ds((1 - y) * WIN, HALF), :] = jnp.zeros((2, HALF, 128), jnp.float32)
+
+    def add_returned(i):
+        g = back_head(i - LAG)
+
+        @pl.when(jnp.logical_not(ends))
+        def _():
+            r2(g).wait_recv()
+            gacc[g, :, pl.ds(2 * BLK, BLK), :] += xbuf[g].astype(jnp.float32)
+
+        @pl.when(lax.div(g, 4) != y)
+        def _():
+            m = lax.rem(g, 4)
+            r1buf[m] = gacc[g, :, pl.ds(2 * BLK, BLK), :].astype(jnp.bfloat16)
+            r1(m).start()
 
     def stage(i, carry):
         @pl.when(i < OWN_HEADS)
@@ -209,6 +227,12 @@
             def _():
                 f3(slot(g, 0), g).start()
 
+        early = (core == 1) & (i >= 0)
+
+        @pl.when((i >= LAG) & early)
+        def _():
+            add_returned(i)
+
         @pl.when((i >= 1) & (i < 9))
         def _():
             g = stage_head(i - 1)
@@ -223,20 +247,9 @@
             def _():
                 gacc[g, :, pl.ds(2 * BLK, BLK), :] += dbuf[g].astype(jnp.float32)
 
-        @pl.when(i >= LAG)
-        def _():
-            g = back_head(i - LAG)
-
-            @pl.when(jnp.logical_not(ends))
-            def _():
-                r2(g).wait_recv()
-                gacc[g, :, pl.ds(2 * BLK, BLK), :] += xbuf[g].astype(jnp.float32)
-
-            @pl.when(lax.div(g, 4) != y)
-            def _():
-                m = lax.rem(g, 4)
-                r1buf[m] = gacc[g, :, pl.ds(2 * BLK, BLK), :].astype(jnp.bfloat16)
-                r1(m).start()
+        @pl.when((i >= LAG) & jnp.logical_not(early))
+        def _():
+            add_returned(i)
 
         @pl.when(i < HEADS)
         def _():
@@ -322,6 +335,7 @@
             pltpu.VMEM((HEADS, GROUP, 128), bf),
             pltpu.VMEM((HEADS, GROUP, 128), bf),
             pltpu.VMEM((HEADS, GROUP, 128), bf),
+            pltpu.VMEM((HEADS, 1, GROUP), f32),
             pltpu.VMEM((HEADS, 1, GROUP), f32),
             pltpu.VMEM((HEADS, GROUP, 128), bf),
             pltpu.VMEM((HEADS, 2, 3 * BLK, 128), bf),

time: 57.2 us -> 57 us (level)
  no operation moved by 1% of the time
where the time goes in v3:
time: 57 us; the launch traced here: 56 us
  Pallas kernels  55.3 us (97%)
  between operations  0.64 us (1%)
    pallas_call x1, Pallas kernels, attention_grads(): pl.pallas_call(lambda *refs: kernel(n_seq, *refs), out_shape=shapes, in_s...  53.9 us
    pallas_call x1, Pallas kernels, attention_grads(): pl.pallas_call(store, out_shape=shapes, in_specs=[vm] * 3, out_specs=(hbm...  1.42 us

profile of v3, /device:TPU:119, one launch (start us, length us, event | category | flops | bytes accessed | tf_op | source)
XLA Modules:
  0.0 56.0 jit_solution(3195281096227155248)
XLA Ops:
  0.6 53.9 %window_grads.1 = (bf16[192,32,128]{2,1,0:T(8,128)(2,1)S(1)}, bf16[384,4,128]{2,1,0:T(4,128)(2,1)S(1)}, bf16[384,4,128]{2,1,0:T(4,128)(2,1)S(1)}) custom-call(bf16[384,4,128]{2,1,0:T(4,128)(2,1)} %refs_0_.1, bf16[384,4,128]{2,1,0:T(4,128)(2,1)} %refs_1_.1, bf16[192,32,128]{2,1,0:T(8,128)(2,1)} %refs_2_.1, bf16[192,32,128]{2,1,0:T(8,128)(2,1)} %refs_3_.1, ...), custom_call_target="tpu_custom_call" | custom-call | tf_op jit(solution)/shard_map/window_grads/pallas_call | solution.py:322
  54.5 1.4 %store_grads.1 = (bf16[192,32,128]{2,1,0:T(8,128)(2,1)}, bf16[384,4,128]{2,1,0:T(4,128)(2,1)}, bf16[384,4,128]{2,1,0:T(4,128)(2,1)}) custom-call(bf16[192,32,128]{2,1,0:T(8,128)(2,1)S(1)} %get-tuple-element.6.a_ref, bf16[384,4,128]{2,1,0:T(4,128)(2,1)S(1)} %get-tuple-element.7.b_ref, bf16[384,4,128]{2,1,0:T(4,128)(2,1)S(1)} %get-tuple-element.8.c_ref), custom_call_target="tpu_custom_call" | custom-call | tf_op jit(solution)/shard_map/store_grads/pallas_call | solution.py:357
